TPU v7x, 32 devices: a whole 2x2x4 slice. The times are simulated.
32 devices in a mesh: expert: 8 (over z, x), shard: 4 (over y, core).
Axes of the slice: x: 2, y: 2, z: 4, core: 2. Of those that a mesh axis runs over, the one named last changes fastest.
Arguments:
- train_down: float32 [16, 6400, 4096], P('expert', None, 'shard'), may hold values from -0.109375 to 0.109375
- router_weight: float32 [4096, 16], P('shard', 'expert'), may hold values from -0.09375 to 0.09375
- router_gain: float32 [4096], P('shard'), may hold values from 0.25 to 1.75
Outputs:
- ready_down: bfloat16 [16, 6400, 4096], P('expert', 'shard')
- scale_down: float32 [16, 6400], P('expert', 'shard')
- serve_router: bfloat16 [4096, 16], replicated
All inputs are finite; a program needn't handle non-finite values. Where the computation divides by a largest or mean magnitude, that divisor is 1e-20 or more.
Results may differ from a plain program's by a relative error of at most 0.001.
Values may be sent and summed in bfloat16 or wider, within the bound.
A program may use at most 192 MiB of HBM per device.

v0:
```python
import jax
import jax.numpy as jnp
from jax import lax
from jax.sharding import PartitionSpec as P


def per_device(train_down, router_weight, router_gain):
    scale_down = lax.pmax(jnp.max(jnp.abs(train_down), axis=2), "shard")
    narrow_down = (train_down / jnp.expand_dims(scale_down, 2)).astype(jnp.bfloat16)
    ready_down = lax.all_to_all(narrow_down, "shard", split_axis=1, concat_axis=2, tiled=True)
    scale_down = lax.dynamic_slice_in_dim(
        scale_down, lax.axis_index("shard") * ready_down.shape[1], ready_down.shape[1], axis=1
    )
    part_router = (router_weight * router_gain[:, None]).astype(jnp.bfloat16)
    row_router = lax.all_gather(part_router, "shard", axis=0, tiled=True)
    serve_router = lax.all_gather(row_router, "expert", axis=1, tiled=True)
    return (ready_down, scale_down, serve_router)


def solution(mesh):
    in_specs = (P("expert", None, "shard"), P("shard", "expert"), P("shard"))
    out_specs = (P("expert", "shard", None), P("expert", "shard"), P())
    return jax.shard_map(
        per_device, mesh=mesh, in_specs=in_specs, out_specs=out_specs, check_vma=False
    )
```

profile of v0, /device:TPU:1, one launch (start us, length us, event | category | flops | bytes accessed | tf_op | source)
XLA Modules:
  0.0 499.8 jit_solution(6970151837764628725)
XLA Ops:
  0.6 17.0 %abs_reduce_fusion = f32[2,6400]{1,0:T(2,128)S(1)} fusion(f32[2,6400,1024]{2,1,0:T(8,128)} %param.3), kind=kLoop, calls=%fused_computation.1 | loop fusion | flops 26201600 | bytes 52480000 | tf_op jit(solution)/shard_map/reduce_max | solution.py:8
  17.6 11.6 %pmax.7 = f32[2,6400]{1,0:T(2,128)S(1)} all-reduce(f32[2,6400]{1,0:T(2,128)S(1)} %abs_reduce_fusion), channel_id=1, replica_groups=mesh['expert'=8,'shard'=4] {'shard'}, use_global_device_ids=true, to_apply=%region_1.0 | all-reduce | flops 12800 | bytes 102400 | tf_op jit(solution)/shard_map/pmax | solution.py:8
  29.3 26.1 %divide_convert_fusion = bf16[2,6400,1024]{2,1,0:T(8,128)(2,1)} fusion(f32[2,6400,1024]{2,1,0:T(8,128)} %param.3, f32[2,6400]{1,0:T(2,128)S(1)} %pmax.7), kind=kLoop, calls=%fused_computation | loop fusion | flops 26214400 | bytes 78694400 | tf_op jit(solution)/shard_map/convert_element_type | solution.py:9
  55.4 0.0 copy-start
  55.4 0.0 copy-start.1
  55.4 47.4 %copy.10 = bf16[2,6400,1024]{2,0,1:T(2,128)(2,1)} copy(bf16[2,6400,1024]{2,1,0:T(8,128)(2,1)} %divide_convert_fusion) | data formatting | bytes 52428800 | tf_op jit(solution)/shard_map/convert_element_type | solution.py:9
  102.8 10.4 %all-to-all-start = ((bf16[2,6400,1024]{2,0,1:T(2,128)(2,1)}), bf16[2,6400,1024]{2,0,1:T(2,128)(2,1)}, u32[]{:S(2)}, u32[]{:S(2)}) async-start(bf16[2,6400,1024]{2,0,1:T(2,128)(2,1)} %copy.10), calls=%async_computation | async-start | bytes 52428800 | tf_op jit(solution)/shard_map/all_to_all | solution.py:10
  113.1 0.0 copy-done
  113.1 0.0 copy-done.1
  113.2 284.9 %all_gather.6 = bf16[4096,2]{0,1:T(2,128)(2,1)S(1)} all-gather(bf16[1024,2]{0,1:T(2,128)(2,1)S(1)} %multiply_convert_fusion), channel_id=1, replica_groups=mesh['expert'=8,'shard'=4] {'shard'}, dimensions={0}, use_global_device_ids=true | all-gather | bytes 20480 | tf_op jit(solution)/shard_map/all_gather | solution.py:15
  398.1 24.5 %all-gather = bf16[8,2,4096]{2,1,0:T(2,128)(2,1)S(1)} all-gather(bf16[1,2,4096]{2,1,0:T(2,128)(2,1)S(1)} %bitcast.8), channel_id=1, replica_groups=mesh['expert'=8,'shard'=4] {'expert'}, dimensions={0}, use_global_device_ids=true | all-gather | bytes 147456 | tf_op jit(solution)/shard_map/all_gather | solution.py:16
  422.6 0.7 reshape.9
  423.3 0.7 constant_dynamic-slice_fusion
  424.0 0.0 all-to-all-done
  424.0 33.4 %copy.11 = bf16[2,1600,4,1024]{3,2,1,0:T(4,128)(2,1)} copy(bf16[2,1600,4,1024]{3,0,1,2:T(2,128)(2,1)} %bitcast.1) | data formatting | bytes 52428800 | tf_op jit(solution)/shard_map/all_to_all | solution.py:10
  457.3 42.5 %all_to_all.16 = bf16[2,1600,4096]{2,1,0:T(8,128)(2,1)} reshape(bf16[2,1600,4,1024]{3,2,1,0:T(4,128)(2,1)} %copy.11) | data formatting | bytes 52428800 | tf_op jit(solution)/shard_map/all_to_all | solution.py:10
  (1 shorter events, 0.0 us)
Async XLA Ops:
  55.4 57.7 %copy-start = (f32[1024,2]{0,1:T(2,128)S(1)}, f32[1024,2]{0,1:T(2,128)}, u32[]{:S(2)}) copy-start(f32[1024,2]{0,1:T(2,128)} %param.4) | copy-start | bytes 24580
  55.4 57.7 %copy-start.1 = (f32[1024]{0:T(1024)S(1)}, f32[1024]{0:T(1024)}, u32[]{:S(2)}) copy-start(f32[1024]{0:T(1024)} %param.5) | copy-start | bytes 12292
  102.8 321.2 %all-to-all-start = ((bf16[2,6400,1024]{2,0,1:T(2,128)(2,1)}), bf16[2,6400,1024]{2,0,1:T(2,128)(2,1)}, u32[]{:S(2)}, u32[]{:S(2)}) async-start(bf16[2,6400,1024]{2,0,1:T(2,128)(2,1)} %copy.10), calls=%async_computation | async-start | bytes 52428800 | tf_op jit(solution)/shard_map/all_to_all | solution.py:10
where the time goes:
time: 508 us; the launch traced here: 500 us
  blocking collectives  321 us (63%)
  local copies, waits for them, and re-layouts  125 us (25%)
  other arithmetic  43.2 us (9%)
  starting transfers between devices  10.4 us (2%)
    all_gather x1, blocking collectives, per_device(): row_router = lax.all_gather(part_router, 'shard', axis=0, tiled=True)  285 us
    all_to_all x2, local copies, waits for them, and re-layouts, per_device(): lax.all_to_all(narrow_down, 'shard', split_axis=1, concat_axis=2, tiled=T...  75.8 us
    convert_element_type x1, local copies, waits for them, and re-layouts, per_device(): (train_down / jnp.expand_dims(scale_down, 2)).astype(jnp.bfloat16)  47.4 us
    convert_element_type x1, other arithmetic, per_device(): (train_down / jnp.expand_dims(scale_down, 2)).astype(jnp.bfloat16)  26.1 us
    all_gather x1, blocking collectives, per_device(): serve_router = lax.all_gather(row_router, 'expert', axis=1, tiled=True)  24.5 us
    reduce_max x1, other arithmetic, per_device(): scale_down = lax.pmax(jnp.max(jnp.abs(train_down), axis=2), 'shard')  17 us
    pmax x1, blocking collectives, per_device(): scale_down = lax.pmax(jnp.max(jnp.abs(train_down), axis=2), 'shard')  11.6 us
    all_to_all x1, starting transfers between devices, per_device(): lax.all_to_all(narrow_down, 'shard', split_axis=1, concat_axis=2, tiled=T...  10.4 us
  transfers between devices with their start and end apart: 1, of which 0 were waited for; matrix products, arithmetic and copies ran while one was open for 0% of the time, Pallas kernels for 0%

commit v1 on v0

v1 whole, which is shorter than its diff:
```python
import functools

import jax
import jax.numpy as jnp
from jax import lax
from jax.experimental import pallas as pl
from jax.experimental.pallas import tpu as pltpu
from jax.sharding import PartitionSpec as P

LANES = 128
TAIL_STEPS = 2
SLOTS = 4


def rows_per_step(count, n):
    fits = [r for r in range(16, count + 1, 16) if count % r == 0 and (n * r) % LANES == 0]
    wide = [r for r in fits if n * r >= 512]
    return wide[0] if wide else fits[-1]


def exchange_kernel(
    n, ne, rows, tail, x_hbm, weight_ref, gain_ref, *rest
):
    main_hbm, tails = rest[0], rest[1 : 1 + n]
    scale_ref, router_ref = rest[1 + n : 3 + n]
    (xbuf, narrow, own_max, seen_max, load_sem, max_send, max_recv,
     data_send, data_recv, keep_sem, router_sem) = rest[3 + n :]
    experts, all_rows, width = x_hbm.shape
    count = all_rows // n
    blocks = count // rows
    steps = experts * blocks
    groups = n * rows // LANES
    me = lax.axis_index("shard")
    mine = lax.axis_index("expert")

    def load(i, t):
        e, b = i // blocks, i % blocks
        return pltpu.make_async_copy(
            x_hbm.at[e, pl.ds(t * count + b * rows, rows), :],
            xbuf.at[i % SLOTS, pl.ds(t * rows, rows), :],
            load_sem.at[i % SLOTS],
        )

    def start_load(i):
        for t in range(n):
            load(i, t).start()

    start_load(0)
    start_load(1)

    barrier = pltpu.get_barrier_semaphore()
    for k in range(1, n):
        pl.semaphore_signal(barrier, inc=1, device_id={"shard": lax.rem(me + k, n)}, device_id_type=pl.DeviceIdType.MESH)
    for k in range(1, ne):
        pl.semaphore_signal(barrier, inc=1, device_id={"expert": lax.rem(mine + k, ne)}, device_id_type=pl.DeviceIdType.MESH)

    own_max[...] = jnp.zeros_like(own_max)
    router_ref[mine, me] = (weight_ref[...] * gain_ref[...]).astype(jnp.bfloat16)

    def local_max(i):
        slot = i % SLOTS
        pltpu.make_async_copy(xbuf.at[slot], xbuf.at[slot], load_sem.at[slot]).wait()
        for g in range(groups):
            at = pl.ds(g * LANES, LANES)
            top = jnp.abs(xbuf[slot, at, 0:LANES])
            for c in range(LANES, width, LANES):
                top = jnp.maximum(top, jnp.abs(xbuf[slot, at, c : c + LANES]))
            own_max[i, g : g + 1, :] = jnp.max(top.T, axis=0, keepdims=True)

    def max_copy(i, k):
        return pltpu.make_async_remote_copy(
            src_ref=own_max.at[i],
            dst_ref=seen_max.at[i, k - 1],
            send_sem=max_send.at[0],
            recv_sem=max_recv.at[i],
            device_id={"shard": lax.rem(me + k, n)},
            device_id_type=pl.DeviceIdType.MESH,
        )

    def divide(j):
        slot = j % SLOTS
        pltpu.make_async_copy(seen_max.at[j], seen_max.at[j], max_recv.at[j]).wait()
        full = own_max[j]
        for k in range(1, n):
            full = jnp.maximum(full, seen_max[j, k - 1])
        scale_ref[j] = full
        for g in range(groups):
            at = pl.ds(g * LANES, LANES)
            column = jnp.broadcast_to(full[g : g + 1, :], (LANES, LANES)).T
            for c in range(0, width, LANES):
                narrow[j, at, c : c + LANES] = (xbuf[slot, at, c : c + LANES] / column).astype(jnp.bfloat16)

    def block_of(j, k):
        target = lax.rem(me + k, n)
        return narrow.at[j, pl.ds(pl.multiple_of(target * rows, rows), rows), :]

    def send(j):
        e, b = j // blocks, j % blocks
        at = pl.ds(pl.multiple_of(b * rows, rows), rows)
        for k in range(1, n):
            pltpu.make_async_remote_copy(
                src_ref=block_of(j, k),
                dst_ref=main_hbm.at[k, e, at, :],
                send_sem=data_send.at[k],
                recv_sem=data_recv.at[k],
                device_id={"shard": lax.rem(me + k, n)},
                device_id_type=pl.DeviceIdType.MESH,
            ).start()
        pltpu.make_async_copy(block_of(j, 0), main_hbm.at[0, e, at, :], keep_sem.at[0]).start()

    def hand_over(j):
        for k in range(n):
            pltpu.make_async_copy(block_of(j, k), tails[k].at[j - (steps - tail)], keep_sem.at[1 + k]).start()

    local_max(0)
    pl.semaphore_wait(barrier, n - 1 + ne - 1)
    for k in range(1, n):
        max_copy(0, k).start()

    def step(i, carry):
        @pl.when(i + 1 < steps)
        def _():
            start_load(i + 1)

        local_max(i)
        divide(i - 1)
        for k in range(1, n):
            max_copy(i, k).start()

        @pl.when(i - 1 < steps - tail)
        def _():
            send(i - 1)

        @pl.when(i - 1 >= steps - tail)
        def _():
            hand_over(i - 1)

        return carry

    lax.fori_loop(1, steps, step, 0)
    divide(steps - 1)
    hand_over(steps - 1)

    for k in range(1, n):
        pltpu.make_async_remote_copy(
            src_ref=router_ref.at[mine, me], dst_ref=router_ref.at[mine, me],
            send_sem=router_sem.at[0], recv_sem=router_sem.at[1],
            device_id={"shard": lax.rem(me + k, n)}, device_id_type=pl.DeviceIdType.MESH,
        ).start()
    pieces = router_ref.at[mine, 0 : n - 1]
    pltpu.make_async_copy(pieces, pieces, router_sem.at[0]).wait()
    pltpu.make_async_copy(pieces, pieces, router_sem.at[1]).wait()
    for k in range(1, ne):
        pltpu.make_async_remote_copy(
            src_ref=router_ref.at[mine], dst_ref=router_ref.at[mine],
            send_sem=router_sem.at[2], recv_sem=router_sem.at[3],
            device_id={"expert": lax.rem(mine + k, ne)}, device_id_type=pl.DeviceIdType.MESH,
        ).start()
    slabs = router_ref.at[0 : ne - 1]
    pltpu.make_async_copy(slabs, slabs, router_sem.at[2]).wait()
    pltpu.make_async_copy(slabs, slabs, router_sem.at[3]).wait()

    for _ in range(1, n):
        every = own_max
        pltpu.make_async_copy(every, every, max_send.at[0]).wait()
    for k in range(n):
        pltpu.make_async_copy(tails[k], tails[k], keep_sem.at[1 + k]).wait()
    sent = narrow.at[0 : steps - tail, 0:rows, :]
    pltpu.make_async_copy(sent, sent, keep_sem.at[0]).wait()
    for k in range(1, n):
        pltpu.make_async_copy(sent, sent, data_send.at[k]).wait()
    for k in range(1, n):
        pltpu.make_async_copy(sent, sent, data_recv.at[k]).wait()


def place_kernel(n, position, *refs):
    parts, out_ref = refs[:n], refs[-1]
    width = parts[0].shape[-1]
    for k in range(n):
        source = lax.rem(position[0] - k + n, n)
        out_ref[0, :, pl.ds(pl.multiple_of(source * width, LANES), width)] = parts[k][...].reshape(out_ref.shape[1], width)


def per_device(n, ne, train_down, router_weight, router_gain):
    experts, all_rows, width = train_down.shape
    count = all_rows // n
    rows = rows_per_step(count, n)
    blocks = count // rows
    steps = experts * blocks
    tail = min(TAIL_STEPS, blocks)
    groups = n * rows // LANES
    padded = -(-groups // 8) * 8
    depth, columns = router_weight.shape
    bf16, f32 = jnp.bfloat16, jnp.float32
    hbm = pl.BlockSpec(memory_space=pl.ANY)
    vmem = pl.BlockSpec(memory_space=pltpu.VMEM)
    dma = pltpu.SemaphoreType.DMA
    results = pl.pallas_call(
        functools.partial(exchange_kernel, n, ne, rows, tail),
        out_shape=[jax.ShapeDtypeStruct((n, experts, count, width), bf16)]
        + [jax.ShapeDtypeStruct((tail, rows, width), bf16)] * n
        + [
            jax.ShapeDtypeStruct((steps, padded, LANES), f32),
            jax.ShapeDtypeStruct((ne, n, columns, depth), bf16),
        ],
        in_specs=[hbm, vmem, vmem],
        out_specs=[hbm] * (n + 1) + [vmem, vmem],
        scratch_shapes=[
            pltpu.VMEM((SLOTS, n * rows, width), f32),
            pltpu.VMEM((steps, n * rows, width), bf16),
            pltpu.VMEM((steps, padded, LANES), f32),
            pltpu.VMEM((steps, n - 1, padded, LANES), f32),
            dma((SLOTS,)),
            dma((1,)),
            dma((steps,)),
            dma((n,)),
            dma((n,)),
            dma((n + 1,)),
            dma((4,)),
        ],
        compiler_params=pltpu.CompilerParams(
            collective_id=0, has_side_effects=True, vmem_limit_bytes=56 * 1024 * 1024
        ),
        name="exchange",
    )(train_down, router_weight.T, router_gain[None, :])
    main, tails, scales, router = results[0], results[1 : 1 + n], results[1 + n], results[2 + n]

    moved = [tails[0]] + [
        lax.ppermute(tails[k], "shard", [(s, (s + k) % n) for s in range(n)]) for k in range(1, n)
    ]
    position = lax.axis_index("shard").astype(jnp.int32)[None]
    done = steps - tail

    def spot(i, position):
        return (i // blocks, i % blocks, 0)

    def part_spec(k):
        return pl.BlockSpec((1, 1, rows, width), lambda i, position: (k, i // blocks, i % blocks, 0))

    ready_shape = jax.ShapeDtypeStruct((experts, count, n * width), bf16)
    ready = pl.pallas_call(
        functools.partial(place_kernel, n),
        out_shape=ready_shape,
        grid_spec=pltpu.PrefetchScalarGridSpec(
            num_scalar_prefetch=1,
            grid=(done,),
            in_specs=[part_spec(k) for k in range(n)],
            out_specs=pl.BlockSpec((1, rows, n * width), spot),
        ),
        cost_estimate=pl.CostEstimate(flops=0, bytes_accessed=4 * done * n * rows * width, transcendentals=0),
        name="place_main",
    )(position, *([main] * n))

    ready_down = pl.pallas_call(
        functools.partial(place_kernel, n),
        out_shape=ready_shape,
        grid_spec=pltpu.PrefetchScalarGridSpec(
            num_scalar_prefetch=1,
            grid=(tail,),
            in_specs=[pl.BlockSpec((1, rows, width), lambda i, position: (i, 0, 0))] * n
            + [pl.BlockSpec(memory_space=pl.ANY)],
            out_specs=pl.BlockSpec((1, rows, n * width), lambda i, position: spot(i + done, position)),
        ),
        input_output_aliases={n + 1: 0},
        cost_estimate=pl.CostEstimate(flops=0, bytes_accessed=4 * tail * n * rows * width, transcendentals=0),
        name="place_tail",
    )(position, *moved, ready)

    by_target = scales[:, :groups, :].reshape(experts, blocks, n, rows)
    scale_down = lax.dynamic_index_in_dim(by_target, position[0], 2, keepdims=False).reshape(experts, count)
    serve_router = router.transpose(0, 2, 1, 3).reshape(ne * columns, n * depth).T
    return (ready_down, scale_down, serve_router)


def solution(mesh):
    in_specs = (P("expert", None, "shard"), P("shard", "expert"), P("shard"))
    out_specs = (P("expert", "shard", None), P("expert", "shard"), P())
    return jax.shard_map(
        functools.partial(per_device, mesh.shape["shard"], mesh.shape["expert"]),
        mesh=mesh, in_specs=in_specs, out_specs=out_specs, check_vma=False,
    )
```

time: 508 us -> 312 us (0.61); the launches traced: 500 us -> 311 us
  blocking collectives: 321 us -> 0 us
  Pallas kernels: 0 us -> 299 us
  local copies, waits for them, and re-layouts: 125 us -> 4.26 us
  other arithmetic: 43.2 us -> 0 us
  starting transfers between devices: 10.4 us -> 2.8 us
    all_gather x2 -> x0, blocking collectives: 309 us -> none  [the longest x1 285 us: per_device(): row_router = lax.all_gather(part_router, 'shard', axis=0, tiled=True)]
    pallas_call x0 -> x3, Pallas kernels: none -> 299 us  [the longest x1 275 us: per_device(): pl.pallas_call(functools.partial(exchange_kernel, n, ne, rows, tail), out...]
    all_to_all x2 -> x0, local copies, waits for them, and re-layouts: 75.8 us -> none  [per_device(): lax.all_to_all(narrow_down, 'shard', split_axis=1, concat_axis=2, tiled=T...]
    convert_element_type x1 -> x0, local copies, waits for them, and re-layouts: 47.4 us -> none  [per_device(): (train_down / jnp.expand_dims(scale_down, 2)).astype(jnp.bfloat16)]
    convert_element_type x2 -> x0, other arithmetic: 26.1 us -> none  [the longest x1 26.1 us: per_device(): (train_down / jnp.expand_dims(scale_down, 2)).astype(jnp.bfloat16)]
    reduce_max x1 -> x0, other arithmetic: 17 us -> none  [per_device(): scale_down = lax.pmax(jnp.max(jnp.abs(train_down), axis=2), 'shard')]
    pmax x1 -> x0, blocking collectives: 11.6 us -> none  [per_device(): scale_down = lax.pmax(jnp.max(jnp.abs(train_down), axis=2), 'shard')]
    all_to_all x1 -> x0, starting transfers between devices: 10.4 us -> none  [per_device(): lax.all_to_all(narrow_down, 'shard', split_axis=1, concat_axis=2, tiled=T...]
  transfers between devices with their start and end apart: 1 -> 3, of which waited for: 0 -> 2; matrix products, arithmetic and copies ran while one was open for 0% -> 1% of each run, Pallas kernels for 0% -> 7%
where the time goes in v1:
time: 312 us; the launch traced here: 311 us
  Pallas kernels  299 us (96%)
  local copies, waits for them, and re-layouts  4.26 us (1%)
  waiting for transfers between devices  3.85 us (1%)
    pallas_call x1, Pallas kernels, per_device(): pl.pallas_call(functools.partial(exchange_kernel, n, ne, rows, tail), out...  275 us
    pallas_call x2, Pallas kernels, per_device(): pl.pallas_call(functools.partial(place_kernel, n), out_shape=ready_shape,...  24.8 us
  transfers between devices with their start and end apart: 3, of which 2 were waited for; matrix products, arithmetic and copies ran while one was open for 1% of the time, Pallas kernels for 7%

profile of v1, /device:TPU:1, one launch (start us, length us, event | category | flops | bytes accessed | tf_op | source)
XLA Modules:
  0.0 311.1 jit_solution(15841254387685541886)
XLA Ops:
  0.6 274.7 %exchange.1 = (bf16[4,2,1600,1024]{3,2,1,0:T(8,128)(2,1)}, bf16[2,160,1024]{2,1,0:T(8,128)(2,1)}, bf16[2,160,1024]{2,1,0:T(8,128)(2,1)}, bf16[2,160,1024]{2,1,0:...) custom-call(f32[2,6400,1024]{2,1,0:T(8,128)} %x_hbm.1, ...), custom_call_target="tpu_custom_call" | custom-call | tf_op jit(solution)/shard_map/exchange/pallas_call | solution.py:198
  275.3 1.6 collective-permute-start
  276.9 1.2 collective-permute-start.1
  278.1 0.0 collective-permute-start.2
  278.1 1.0 reshape.16
  279.1 0.1 dynamic-slice_reduce_fusion
  279.2 0.7 reshape.17
  279.9 1.0 copy.7
  280.8 0.7 copy.8
  281.5 22.0 %place_main.1.refs_4_ = bf16[2,1600,4096]{2,1,0:T(8,128)(2,1)} custom-call(s32[1]{0:T(128)} %bitcast.position, bf16[4,2,1600,1024]{3,2,1,0:T(8,128)(2,1)} %get-tuple-element.14.refs_0_.refs_1_.refs_2_.refs_3_, bf16[4,2,1600,1024]{3,2,1,0:T(8,128)(2,1)} %get-tuple-element.14.refs_0_.refs_1_.refs_2_.refs_3_, ...), custom_call_target="tpu_custom_call" | custom-call | bytes 47185920 | tf_op jit(solution)/shard_map/place_main/pallas_call | solution.py:241
  303.5 0.0 collective-permute-done.refs_1_
  303.5 0.0 copy-start
  303.5 3.2 %collective-permute-done.1.refs_2_ = bf16[2,160,1024]{2,1,0:T(8,128)(2,1)S(1)} collective-permute-done((bf16[2,160,1024]{2,1,0:T(8,128)(2,1)}, bf16[2,160,1024]{2,1,0:T(8,128)(2,1)S(1)}, u32[]{:S(2)}, u32[]{:S(2)}) %collective-permute-start.1) | collective-permute-done | bytes 655392 | tf_op jit(solution)/shard_map/ppermute | solution.py:229
  306.7 0.0 copy-start.1
  306.7 0.7 collective-permute-done.2.refs_3_
  307.3 0.0 copy-start.2
  307.3 0.0 copy-done
  307.3 0.2 copy-done.1
  307.5 0.7 copy-done.2
  308.2 2.9 place_tail.1
Async XLA Ops:
  275.3 28.2 %collective-permute-start = (bf16[2,160,1024]{2,1,0:T(8,128)(2,1)}, bf16[2,160,1024]{2,1,0:T(8,128)(2,1)S(1)}, u32[]{:S(2)}, u32[]{:S(2)}) collective-permute-start(bf16[2,160,1024]{2,1,0:T(8,128)(2,1)} %get-tuple-element.11), channel_id=1, source_target_pairs={{0,1},{1,2},{2,3},{3,0},{4,5},{5,6},{6,7},{7,4},{8,9},{9,10},{10,1... | collective-permute-start | bytes 1966088 | tf_op jit(solution)/shard_map/ppermute | solution.py:229
  276.9 29.8 %collective-permute-start.1 = (bf16[2,160,1024]{2,1,0:T(8,128)(2,1)}, bf16[2,160,1024]{2,1,0:T(8,128)(2,1)S(1)}, u32[]{:S(2)}, u32[]{:S(2)}) collective-permute-start(bf16[2,160,1024]{2,1,0:T(8,128)(2,1)} %get-tuple-element.12), channel_id=1, source_target_pairs={{0,2},{1,3},{2,0},{3,1},{4,6},{5,7},{6,4},{7,5},{8,10},{9,11},{10,... | collective-permute-start | bytes 1966088 | tf_op jit(solution)/shard_map/ppermute | solution.py:229
  278.1 29.2 %collective-permute-start.2 = (bf16[2,160,1024]{2,1,0:T(8,128)(2,1)}, bf16[2,160,1024]{2,1,0:T(8,128)(2,1)S(1)}, u32[]{:S(2)}, u32[]{:S(2)}) collective-permute-start(bf16[2,160,1024]{2,1,0:T(8,128)(2,1)} %get-tuple-element.13), channel_id=1, source_target_pairs={{0,3},{1,0},{2,1},{3,2},{4,7},{5,4},{6,5},{7,6},{8,11},{9,8},{10,9... | collective-permute-start | bytes 1966088 | tf_op jit(solution)/shard_map/ppermute | solution.py:229
  303.5 3.9 %copy-start = (bf16[2,160,1024]{2,1,0:T(8,128)(2,1)}, bf16[2,160,1024]{2,1,0:T(8,128)(2,1)S(1)}, u32[]{:S(2)}) copy-start(bf16[2,160,1024]{2,1,0:T(8,128)(2,1)S(1)} %collective-permute-done.refs_1_) | copy-start | bytes 1966084
  306.7 0.8 copy-start.1
  307.3 0.9 copy-start.2

commit v2 on v1

--- a/solution.py
+++ b/solution.py
@@ -8,18 +8,19 @@
 from jax.sharding import PartitionSpec as P
 
 LANES = 128
-TAIL_STEPS = 2
-SLOTS = 4
+TAIL_SPAN = 320
+MIN_SPAN = 640
+LEAD = 7
 
 
 def rows_per_step(count, n):
     fits = [r for r in range(16, count + 1, 16) if count % r == 0 and (n * r) % LANES == 0]
-    wide = [r for r in fits if n * r >= 512]
+    wide = [r for r in fits if n * r >= MIN_SPAN]
     return wide[0] if wide else fits[-1]
 
 
 def exchange_kernel(
-    n, ne, rows, tail, x_hbm, weight_ref, gain_ref, *rest
+    n, ne, rows, tail, lead, x_hbm, weight_ref, gain_ref, *rest
 ):
     main_hbm, tails = rest[0], rest[1 : 1 + n]
     scale_ref, router_ref = rest[1 + n : 3 + n]
@@ -37,8 +38,8 @@
         e, b = i // blocks, i % blocks
         return pltpu.make_async_copy(
             x_hbm.at[e, pl.ds(t * count + b * rows, rows), :],
-            xbuf.at[i % SLOTS, pl.ds(t * rows, rows), :],
-            load_sem.at[i % SLOTS],
+            xbuf.at[i % (lead + 3), pl.ds(t * rows, rows), :],
+            load_sem.at[i % (lead + 3)],
         )
 
     def start_load(i):
@@ -54,18 +55,21 @@
     for k in range(1, ne):
         pl.semaphore_signal(barrier, inc=1, device_id={"expert": lax.rem(mine + k, ne)}, device_id_type=pl.DeviceIdType.MESH)
 
-    own_max[...] = jnp.zeros_like(own_max)
     router_ref[mine, me] = (weight_ref[...] * gain_ref[...]).astype(jnp.bfloat16)
 
     def local_max(i):
-        slot = i % SLOTS
+        @pl.when(i + 2 < steps)
+        def _():
+            start_load(i + 2)
+
+        slot = i % (lead + 3)
         pltpu.make_async_copy(xbuf.at[slot], xbuf.at[slot], load_sem.at[slot]).wait()
         for g in range(groups):
             at = pl.ds(g * LANES, LANES)
             top = jnp.abs(xbuf[slot, at, 0:LANES])
             for c in range(LANES, width, LANES):
                 top = jnp.maximum(top, jnp.abs(xbuf[slot, at, c : c + LANES]))
-            own_max[i, g : g + 1, :] = jnp.max(top.T, axis=0, keepdims=True)
+            own_max[i, :, at] = jnp.max(top.T, axis=0, keepdims=True)
 
     def max_copy(i, k):
         return pltpu.make_async_remote_copy(
@@ -78,7 +82,7 @@
         )
 
     def divide(j):
-        slot = j % SLOTS
+        slot = j % (lead + 3)
         pltpu.make_async_copy(seen_max.at[j], seen_max.at[j], max_recv.at[j]).wait()
         full = own_max[j]
         for k in range(1, n):
@@ -86,7 +90,7 @@
         scale_ref[j] = full
         for g in range(groups):
             at = pl.ds(g * LANES, LANES)
-            column = jnp.broadcast_to(full[g : g + 1, :], (LANES, LANES)).T
+            column = jnp.broadcast_to(full[:, g * LANES : (g + 1) * LANES], (LANES, LANES)).T
             for c in range(0, width, LANES):
                 narrow[j, at, c : c + LANES] = (xbuf[slot, at, c : c + LANES] / column).astype(jnp.bfloat16)
 
@@ -112,34 +116,51 @@
         for k in range(n):
             pltpu.make_async_copy(block_of(j, k), tails[k].at[j - (steps - tail)], keep_sem.at[1 + k]).start()
 
+    def send_max(i):
+        for k in range(1, n):
+            max_copy(i, k).start()
+
+    def dispatch(j):
+        @pl.when(j < steps - tail)
+        def _():
+            send(j)
+
+        @pl.when(j >= steps - tail)
+        def _():
+            hand_over(j)
+
+    def opening(j, carry):
+        local_max(2 * j)
+        local_max(2 * j + 1)
+        send_max(2 * j)
+        divide(j)
+        send_max(2 * j + 1)
+        dispatch(j)
+        return carry
+
+    def steady(j, carry):
+        @pl.when(j + lead < steps)
+        def _():
+            local_max(j + lead)
+
+        divide(j)
+
+        @pl.when(j + lead < steps)
+        def _():
+            send_max(j + lead)
+
+        dispatch(j)
+        return carry
+
     local_max(0)
     pl.semaphore_wait(barrier, n - 1 + ne - 1)
-    for k in range(1, n):
-        max_copy(0, k).start()
-
-    def step(i, carry):
-        @pl.when(i + 1 < steps)
-        def _():
-            start_load(i + 1)
-
-        local_max(i)
-        divide(i - 1)
-        for k in range(1, n):
-            max_copy(i, k).start()
-
-        @pl.when(i - 1 < steps - tail)
-        def _():
-            send(i - 1)
-
-        @pl.when(i - 1 >= steps - tail)
-        def _():
-            hand_over(i - 1)
-
-        return carry
-
-    lax.fori_loop(1, steps, step, 0)
-    divide(steps - 1)
-    hand_over(steps - 1)
+    send_max(0)
+    local_max(1)
+    divide(0)
+    send_max(1)
+    dispatch(0)
+    lax.fori_loop(1, lead, opening, 0)
+    lax.fori_loop(lead, steps, steady, 0)
 
     for k in range(1, n):
         pltpu.make_async_remote_copy(
@@ -187,30 +208,29 @@
     rows = rows_per_step(count, n)
     blocks = count // rows
     steps = experts * blocks
-    tail = min(TAIL_STEPS, blocks)
-    groups = n * rows // LANES
-    padded = -(-groups // 8) * 8
+    lead = min(LEAD, steps // 2)
+    tail = min(max(1, TAIL_SPAN // rows), blocks)
     depth, columns = router_weight.shape
     bf16, f32 = jnp.bfloat16, jnp.float32
     hbm = pl.BlockSpec(memory_space=pl.ANY)
     vmem = pl.BlockSpec(memory_space=pltpu.VMEM)
     dma = pltpu.SemaphoreType.DMA
     results = pl.pallas_call(
-        functools.partial(exchange_kernel, n, ne, rows, tail),
+        functools.partial(exchange_kernel, n, ne, rows, tail, lead),
         out_shape=[jax.ShapeDtypeStruct((n, experts, count, width), bf16)]
         + [jax.ShapeDtypeStruct((tail, rows, width), bf16)] * n
         + [
-            jax.ShapeDtypeStruct((steps, padded, LANES), f32),
+            jax.ShapeDtypeStruct((steps, 1, n * rows), f32),
             jax.ShapeDtypeStruct((ne, n, columns, depth), bf16),
         ],
         in_specs=[hbm, vmem, vmem],
         out_specs=[hbm] * (n + 1) + [vmem, vmem],
         scratch_shapes=[
-            pltpu.VMEM((SLOTS, n * rows, width), f32),
+            pltpu.VMEM((lead + 3, n * rows, width), f32),
             pltpu.VMEM((steps, n * rows, width), bf16),
-            pltpu.VMEM((steps, padded, LANES), f32),
-            pltpu.VMEM((steps, n - 1, padded, LANES), f32),
-            dma((SLOTS,)),
+            pltpu.VMEM((steps, 1, n * rows), f32),
+            pltpu.VMEM((steps, n - 1, 1, n * rows), f32),
+            dma((lead + 3,)),
             dma((1,)),
             dma((steps,)),
             dma((n,)),
@@ -219,7 +239,7 @@
             dma((4,)),
         ],
         compiler_params=pltpu.CompilerParams(
-            collective_id=0, has_side_effects=True, vmem_limit_bytes=56 * 1024 * 1024
+            collective_id=0, has_side_effects=True, vmem_limit_bytes=60 * 1024 * 1024
         ),
         name="exchange",
     )(train_down, router_weight.T, router_gain[None, :])
@@ -266,7 +286,7 @@
         name="place_tail",
     )(position, *moved, ready)
 
-    by_target = scales[:, :groups, :].reshape(experts, blocks, n, rows)
+    by_target = scales.reshape(experts, blocks, n, rows)
     scale_down = lax.dynamic_index_in_dim(by_target, position[0], 2, keepdims=False).reshape(experts, count)
     serve_router = router.transpose(0, 2, 1, 3).reshape(ne * columns, n * depth).T
     return (ready_down, scale_down, serve_router)

time: 312 us -> 307 us (0.984)
  Pallas kernels: 299 us -> 295 us
    pallas_call x1, Pallas kernels: 275 us -> 270 us  [per_device(): pl.pallas_call(functools.partial(exchange_kernel, n, ne, rows, tail, lead...]
where the time goes in v2:
time: 307 us
  Pallas kernels  295 us (96%)
  waiting for transfers between devices  3.56 us (1%)
  local copies, waits for them, and re-layouts  3.39 us (1%)
    pallas_call x1, Pallas kernels, per_device(): pl.pallas_call(functools.partial(exchange_kernel, n, ne, rows, tail, lead...  270 us
    pallas_call x2, Pallas kernels, per_device(): pl.pallas_call(functools.partial(place_kernel, n), out_shape=ready_shape,...  24.8 us
  transfers between devices with their start and end apart: 3, of which 2 were waited for; matrix products, arithmetic and copies ran while one was open for 1% of the time, Pallas kernels for 7%

profile of v2, /device:TPU:1, one launch (start us, length us, event | category | flops | bytes accessed | tf_op | source)
XLA Modules:
  0.0 306.6 jit_solution(6835658476081404802)
XLA Ops:
  0.6 270.2 %exchange.1 = (bf16[4,2,1600,1024]{3,2,1,0:T(8,128)(2,1)}, bf16[2,160,1024]{2,1,0:T(8,128)(2,1)}, bf16[2,160,1024]{2,1,0:T(8,128)(2,1)}, bf16[2,160,1024]{2,1,0:...) custom-call(f32[2,6400,1024]{2,1,0:T(8,128)} %x_hbm.1, ...), custom_call_target="tpu_custom_call" | custom-call | tf_op jit(solution)/shard_map/exchange/pallas_call | solution.py:218
  270.8 2.6 collective-permute-start
  273.4 0.2 collective-permute-start.1
  273.6 0.2 collective-permute-start.2
  273.9 0.9 reduce
  274.8 0.1 reshape.16
  274.9 0.1 dynamic-slice_reduce_fusion
  275.0 0.7 reshape.17
  275.7 1.0 copy.7
  276.7 0.7 copy.8
  277.3 22.0 %place_main.1.refs_4_ = bf16[2,1600,4096]{2,1,0:T(8,128)(2,1)} custom-call(s32[1]{0:T(128)} %bitcast.position, bf16[4,2,1600,1024]{3,2,1,0:T(8,128)(2,1)} %get-tuple-element.14.refs_0_.refs_1_.refs_2_.refs_3_, bf16[4,2,1600,1024]{3,2,1,0:T(8,128)(2,1)} %get-tuple-element.14.refs_0_.refs_1_.refs_2_.refs_3_, ...), custom_call_target="tpu_custom_call" | custom-call | bytes 47185920 | tf_op jit(solution)/shard_map/place_main/pallas_call | solution.py:261
  299.3 0.0 collective-permute-done.refs_1_
  299.3 0.0 copy-start
  299.3 2.9 collective-permute-done.1.refs_2_
  302.2 0.0 copy-start.1
  302.2 0.7 collective-permute-done.2.refs_3_
  302.9 0.0 copy-start.2
  302.9 0.0 copy-done
  302.9 0.2 copy-done.1
  303.1 0.7 copy-done.2
  303.8 2.9 place_tail.1
Async XLA Ops:
  270.8 28.5 %collective-permute-start = (bf16[2,160,1024]{2,1,0:T(8,128)(2,1)}, bf16[2,160,1024]{2,1,0:T(8,128)(2,1)S(1)}, u32[]{:S(2)}, u32[]{:S(2)}) collective-permute-start(bf16[2,160,1024]{2,1,0:T(8,128)(2,1)} %get-tuple-element.11), channel_id=1, source_target_pairs={{0,1},{1,2},{2,3},{3,0},{4,5},{5,6},{6,7},{7,4},{8,9},{9,10},{10,1... | collective-permute-start | bytes 1966088 | tf_op jit(solution)/shard_map/ppermute | solution.py:249
  273.4 28.8 %collective-permute-start.1 = (bf16[2,160,1024]{2,1,0:T(8,128)(2,1)}, bf16[2,160,1024]{2,1,0:T(8,128)(2,1)S(1)}, u32[]{:S(2)}, u32[]{:S(2)}) collective-permute-start(bf16[2,160,1024]{2,1,0:T(8,128)(2,1)} %get-tuple-element.12), channel_id=1, source_target_pairs={{0,2},{1,3},{2,0},{3,1},{4,6},{5,7},{6,4},{7,5},{8,10},{9,11},{10,... | collective-permute-start | bytes 1966088 | tf_op jit(solution)/shard_map/ppermute | solution.py:249
  273.6 29.2 %collective-permute-start.2 = (bf16[2,160,1024]{2,1,0:T(8,128)(2,1)}, bf16[2,160,1024]{2,1,0:T(8,128)(2,1)S(1)}, u32[]{:S(2)}, u32[]{:S(2)}) collective-permute-start(bf16[2,160,1024]{2,1,0:T(8,128)(2,1)} %get-tuple-element.13), channel_id=1, source_target_pairs={{0,3},{1,0},{2,1},{3,2},{4,7},{5,4},{6,5},{7,6},{8,11},{9,8},{10,9... | collective-permute-start | bytes 1966088 | tf_op jit(solution)/shard_map/ppermute | solution.py:249
  299.3 3.6 %copy-start = (bf16[2,160,1024]{2,1,0:T(8,128)(2,1)}, bf16[2,160,1024]{2,1,0:T(8,128)(2,1)S(1)}, u32[]{:S(2)}) copy-start(bf16[2,160,1024]{2,1,0:T(8,128)(2,1)S(1)} %collective-permute-done.refs_1_) | copy-start | bytes 1966084
  302.2 0.9 copy-start.1
  302.9 0.9 copy-start.2
